TPU v7x, 32 devices: a whole 2x2x4 slice. The times are simulated.
32 devices in a mesh: leaf: 16 (over z, y, core), top: 2 (over x).
Axes of the slice: x: 2, y: 2, z: 4, core: 2. Of those that a mesh axis runs over, the one named last changes fastest.
Arguments:
- vectors: bfloat16 [2, 16, 768, 512], P('top', 'leaf'), may hold values from -6 to 6
- near_tiles: bfloat16 [2, 16, 8, 768, 768], P('top', 'leaf'), may hold values from -0.078125 to 0.078125
- leaf_basis: bfloat16 [2, 16, 768, 128], P('top', 'leaf'), may hold values from -0.21875 to 0.21875
- transfer: bfloat16 [2, 16, 128, 128], P('top', 'leaf'), may hold values from -0.25 to 0.25
- coupling: bfloat16 [2, 16, 7, 128, 128], P('top', 'leaf'), may hold values from -0.1875 to 0.1875
- top_coupling: bfloat16 [2, 2, 128, 128], P('top'), may hold values from -0.375 to 0.375
- near_list: int32 [2, 16, 8], P('top', 'leaf'), may hold values from -4 to 4, as said below
- far_list: int32 [2, 16, 7], P('top', 'leaf'), may hold values from 0 to 15, as said below
- row_counts: int32 [2, 16], P('top', 'leaf'), may hold values from 384 to 768
Outputs:
- product: float32 [2, 16, 768, 512], P('top', 'leaf')
Inputs may be any that keep to these rules, and one draw needn't show every extreme that they name: `near_list`: each leaf's 8 offsets are distinct; an offset that leads outside the cluster's 16 leaves stands for an absent block. `far_list`: each leaf's entries are distinct positions in its cluster, each more than 4 away from the leaf's own position. `row_counts`: rows at and beyond the count are padding.
All inputs are finite; a program needn't handle non-finite values.
Results may differ from a plain program's by a relative error of at most 0.0045.
Values may be sent and summed in bfloat16 or wider, within the bound.
A program may use at most 128 MiB of HBM per device.

v0:
```python
import jax
import jax.numpy as jnp
from jax import lax
from jax.sharding import PartitionSpec as P

REACH = 4


def passed_along(block, axis, distance):
    devices = range(lax.axis_size(axis))
    route = [(i - distance, i) for i in devices if i - distance in devices]
    return lax.ppermute(block, axis, route)


def body(
    vectors,
    near_tiles,
    leaf_basis,
    transfer,
    coupling,
    top_coupling,
    near_list,
    far_list,
    row_counts,
):
    leaf_rows = vectors.shape[2]
    row_index = jnp.arange(leaf_rows, dtype=jnp.int32)
    keep = (row_index < row_counts[0, 0]).astype(jnp.bfloat16)
    masked = vectors[0, 0] * keep[:, None]
    offsets = near_list[0, 0]
    tiles = near_tiles[0, 0]
    window = []
    for offset in range(-REACH, REACH + 1):
        if offset == 0:
            window.append(masked)
        else:
            window.append(passed_along(masked, "leaf", -offset))
    stacked = jnp.stack(window)
    span = jnp.arange(-REACH, REACH + 1, dtype=jnp.int32)
    picker = (offsets[:, None] == span[None, :]).astype(jnp.bfloat16)
    sources = jnp.einsum("kw,wrv->krv", picker, stacked, preferred_element_type=jnp.float32)
    near = jnp.einsum(
        "kij,kjv->iv", tiles, sources.astype(jnp.bfloat16), preferred_element_type=jnp.float32
    )
    basis = leaf_basis[0, 0]
    coeff = jnp.einsum("ir,iv->rv", basis, masked, preferred_element_type=jnp.float32).astype(
        jnp.bfloat16
    )
    nested = transfer[0, 0]
    upward = jnp.einsum("ab,av->bv", nested, coeff, preferred_element_type=jnp.float32)
    clusters = lax.axis_size("top")
    owner = (jnp.arange(clusters, dtype=jnp.int32) == lax.axis_index("top")).astype(jnp.float32)
    parents = lax.psum(owner[:, None, None] * upward[None], ("leaf", "top")).astype(jnp.bfloat16)
    sibling_ids = (lax.axis_index("top") + 1 + jnp.arange(clusters, dtype=jnp.int32)) % clusters
    top_pick = (sibling_ids[:, None] == jnp.arange(clusters, dtype=jnp.int32)[None, :]).astype(
        jnp.bfloat16
    )
    chosen = jnp.einsum(
        "mc,crv->mrv", top_pick, parents, preferred_element_type=jnp.float32
    ).astype(jnp.bfloat16)
    parent_field = jnp.einsum(
        "mab,mbv->av", top_coupling[0], chosen, preferred_element_type=jnp.float32
    ).astype(jnp.bfloat16)
    siblings = far_list[0, 0]
    matrices = coupling[0, 0]
    piece = lax.all_gather(coeff[None], "leaf", axis=0, tiled=True)
    blocks = jnp.arange(piece.shape[0], dtype=jnp.int32)
    chooser = (siblings[:, None] == blocks[None, :]).astype(jnp.bfloat16)
    gathered = jnp.einsum("mn,nrv->mrv", chooser, piece, preferred_element_type=jnp.float32).astype(
        jnp.bfloat16
    )
    local_field = jnp.einsum("mab,mbv->av", matrices, gathered, preferred_element_type=jnp.float32)
    local_field = (
        local_field + jnp.dot(nested, parent_field, preferred_element_type=jnp.float32)
    ).astype(jnp.bfloat16)
    result = near + jnp.dot(basis, local_field, preferred_element_type=jnp.float32)
    result = result * keep[:, None].astype(jnp.float32)
    return result[None, None]


def solution(mesh):
    in_specs = (
        P("top", "leaf", None, None),
        P("top", "leaf", None, None, None),
        P("top", "leaf", None, None),
        P("top", "leaf", None, None),
        P("top", "leaf", None, None, None),
        P("top", None, None, None),
        P("top", "leaf", None),
        P("top", "leaf", None),
        P("top", "leaf"),
    )
    out_specs = P("top", "leaf", None, None)
    return jax.shard_map(body, mesh=mesh, in_specs=in_specs, out_specs=out_specs, check_vma=False)
```

profile of v0, /device:TPU:0, one launch (start us, length us, event | category | flops | bytes accessed | tf_op | source)
XLA Modules:
  0.0 217.3 jit_solution(1711316566224805380)
XLA Ops:
  7.3 1.3 bitcast_multiply_fusion.1
  8.6 5.9 %collective-permute-start = (bf16[768,512]{1,0:T(8,128)(2,1)S(1)}, bf16[768,512]{1,0:T(8,128)(2,1)}, u32[]{:S(2)}, u32[]{:S(2)}) collective-permute-start(bf16[768,512]{1,0:T(8,128)(2,1)S(1)} %bitcast_multiply_fusion.1), channel_id=1, source_target_pairs={{0,8},{2,10},{4,12},{6,14},{8,16},{10,18},{12,20},{14,22},{16,24},... | collective-permute-start | bytes 2359304 | tf_op jit(solution)/shard_map/ppermute | solution.py:12
  14.5 3.5 %collective-permute-start.1 = (bf16[768,512]{1,0:T(8,128)(2,1)S(1)}, bf16[768,512]{1,0:T(8,128)(2,1)}, u32[]{:S(2)}, u32[]{:S(2)}) collective-permute-start(bf16[768,512]{1,0:T(8,128)(2,1)S(1)} %bitcast_multiply_fusion.1), channel_id=1, source_target_pairs={{0,6},{2,8},{4,10},{6,12},{8,14},{10,16},{12,18},{14,20},{16,22},{... | collective-permute-start | bytes 2359304 | tf_op jit(solution)/shard_map/ppermute | solution.py:12
  18.0 3.4 %collective-permute-start.2 = (bf16[768,512]{1,0:T(8,128)(2,1)S(1)}, bf16[768,512]{1,0:T(8,128)(2,1)}, u32[]{:S(2)}, u32[]{:S(2)}) collective-permute-start(bf16[768,512]{1,0:T(8,128)(2,1)S(1)} %bitcast_multiply_fusion.1), channel_id=1, source_target_pairs={{0,4},{2,6},{4,8},{6,10},{8,12},{10,14},{12,16},{14,18},{16,20},{1... | collective-permute-start | bytes 2359304 | tf_op jit(solution)/shard_map/ppermute | solution.py:12
  21.4 2.6 %collective-permute-start.3 = (bf16[768,512]{1,0:T(8,128)(2,1)S(1)}, bf16[768,512]{1,0:T(8,128)(2,1)}, u32[]{:S(2)}, u32[]{:S(2)}) collective-permute-start(bf16[768,512]{1,0:T(8,128)(2,1)S(1)} %bitcast_multiply_fusion.1), channel_id=1, source_target_pairs={{0,2},{2,4},{4,6},{6,8},{8,10},{10,12},{12,14},{14,16},{16,18},{18... | collective-permute-start | bytes 2359304 | tf_op jit(solution)/shard_map/ppermute | solution.py:12
  24.0 1.3 collective-permute-start.4
  25.3 2.4 %convolution_convert_fusion = bf16[512,128]{1,0:T(8,128)(2,1)} fusion(bf16[1,1,768,512]{3,2,1,0:T(8,128)(2,1)} %param.9, bf16[768]{0:T(1024)(128)(2,1)S(1)} %fusion.27, bf16[1,1,768,128]{3,2,1,0:T(8,128)(2,1)} %param.11), kind=kOutput, calls=%fused_computation.15 | convolution fusion | flops 101122048 | bytes 1115648 | tf_op jit(solution)/shard_map/ir,iv->rv/dot_general | solution.py:46
  27.7 1.1 convolution_bitcast_fusion.1
  28.9 0.1 broadcast_multiply_fusion
  29.0 86.0 %all-reduce.1 = bf16[2,128,512]{2,1,0:T(8,128)(2,1)S(1)} all-reduce(f32[2,128,512]{2,1,0:T(8,128)S(1)} %broadcast_multiply_fusion), channel_id=1, replica_groups=mesh['leaf'=16,'top'=2] {'leaf','top'}, use_global_device_ids=true, to_apply=%region_0.0 | all-reduce | flops 131072 | bytes 786432 | tf_op jit(solution)/shard_map/psum | solution.py:53
  115.0 0.5 fusion.18
  115.5 1.1 fusion.11
  116.6 1.3 collective-permute-start.5
  117.9 1.2 bitcast_dynamic-update-slice_fusion.7
  119.1 1.3 collective-permute-start.6
  120.4 1.2 bitcast_dynamic-update-slice_fusion.6
  121.6 1.5 collective-permute-start.7
  123.1 1.2 bitcast_dynamic-update-slice_fusion.5
  124.3 1.2 bitcast_dynamic-update-slice_fusion.4
  125.5 0.2 fusion.15
  125.8 13.1 %collective-permute-done.5 = bf16[768,512]{1,0:T(8,128)(2,1)S(1)} collective-permute-done((bf16[768,512]{1,0:T(8,128)(2,1)S(1)}, bf16[768,512]{1,0:T(8,128)(2,1)S(1)}, u32[]{:S(2)}, u32[]{:S(2)}) %collective-permute-start.5) | collective-permute-done | bytes 786464 | tf_op jit(solution)/shard_map/ppermute | solution.py:12
  139.0 5.5 %collective-permute-done.6 = bf16[768,512]{1,0:T(8,128)(2,1)S(1)} collective-permute-done((bf16[768,512]{1,0:T(8,128)(2,1)S(1)}, bf16[768,512]{1,0:T(8,128)(2,1)S(1)}, u32[]{:S(2)}, u32[]{:S(2)}) %collective-permute-start.6) | collective-permute-done | bytes 786464 | tf_op jit(solution)/shard_map/ppermute | solution.py:12
  144.5 26.2 %collective-permute-done.7 = bf16[768,512]{1,0:T(8,128)(2,1)S(1)} collective-permute-done((bf16[768,512]{1,0:T(8,128)(2,1)S(1)}, bf16[768,512]{1,0:T(8,128)(2,1)S(1)}, u32[]{:S(2)}, u32[]{:S(2)}) %collective-permute-start.7) | collective-permute-done | bytes 786464 | tf_op jit(solution)/shard_map/ppermute | solution.py:12
  170.8 8.7 %fusion = bf16[8,768,512]{2,0,1:T(8,128)(2,1)} fusion(bf16[9,768,512]{2,1,0:T(8,128)(2,1)S(1)} %bitcast_dynamic-update-slice_fusion, s32[9]{0:T(128)S(1)} %iota_add_fusion, s32[8]{0:T(128)S(1)} %bitcast.91), kind=kOutput, calls=%fused_computation | convolution fusion | flops 56623176 | bytes 13369412 | tf_op jit(solution)/shard_map/kw,wrv->krv/dot_general | solution.py:41
  179.4 9.1 %copy.12 = bf16[8,768,512]{1,2,0:T(8,128)(2,1)} copy(bf16[8,768,512]{2,0,1:T(8,128)(2,1)} %fusion) | data formatting | bytes 12582912 | tf_op jit(solution)/shard_map/kw,wrv->krv/dot_general | solution.py:41
  188.5 2.3 %copy.17 = bf16[64,8,16,128]{3,2,1,0:T(8,128)(2,1)S(1)} copy(bf16[64,8,16,128]{3,1,2,0:T(8,128)(2,1)} %bitcast.89) | data formatting | bytes 4194304
  190.8 3.6 %copy.13 = bf16[16,128,512]{2,0,1:T(8,128)(2,1)} copy(bf16[16,128,512]{1,0,2:T(8,128)(2,1)S(1)} %bitcast.88) | data formatting | bytes 4194304 | tf_op jit(solution)/shard_map/all_gather | solution.py:66
  194.3 2.1 fusion.29
  196.4 0.6 convolution_bitcast_fusion.2
  197.0 1.7 fusion.13
  198.7 10.2 %fusion.6 = f32[1,1,768,512]{2,3,1,0:T(8,128)S(1)} fusion(f32[512,768]{1,0:T(8,128)} %fusion.13, bf16[1,1,8,768,768]{4,3,2,1,0:T(8,128)(2,1)} %param.10, bf16[8,768,512]{1,2,0:T(8,128)(2,1)} %copy.12, f32[768]{0:T(1024)S(1)} %fusion.37), kind=kOutput, calls=%fused_computation.8 | convolution fusion | flops 4832624640 | bytes 18877440 | tf_op jit(solution)/shard_map/kij,kjv->iv/dot_general | solution.py:42
  208.9 1.6 copy.10
  (29 shorter events, 0.3 us)
Async XLA Ops:
  6.5 189.9 %copy-start = (bf16[1,1,7,128,128]{4,3,2,1,0:T(8,128)(2,1)S(1)}, bf16[1,1,7,128,128]{4,3,2,1,0:T(8,128)(2,1)}, u32[]{:S(2)}) copy-start(bf16[1,1,7,128,128]{4,3,2,1,0:T(8,128)(2,1)} %param.13) | copy-start | bytes 688132
  6.5 119.0 %copy-start.1 = (bf16[1,1,768,512]{3,2,1,0:T(8,128)(2,1)S(1)}, bf16[1,1,768,512]{3,2,1,0:T(8,128)(2,1)}, u32[]{:S(2)}) copy-start(bf16[1,1,768,512]{3,2,1,0:T(8,128)(2,1)} %param.9) | copy-start | bytes 2359300
  6.5 182.0 %all-gather.3.cloned.1.call-start = ((), (), s32[]{:S(2)}) async-start(), calls=%async_computation | async-start | bytes 2228224 | tf_op jit(solution)/shard_map/all_gather | solution.py:66
  8.6 108.0 %collective-permute-start = (bf16[768,512]{1,0:T(8,128)(2,1)S(1)}, bf16[768,512]{1,0:T(8,128)(2,1)}, u32[]{:S(2)}, u32[]{:S(2)}) collective-permute-start(bf16[768,512]{1,0:T(8,128)(2,1)S(1)} %bitcast_multiply_fusion.1), channel_id=1, source_target_pairs={{0,8},{2,10},{4,12},{6,14},{8,16},{10,18},{12,20},{14,22},{16,24},... | collective-permute-start | bytes 2359304 | tf_op jit(solution)/shard_map/ppermute | solution.py:12
  14.5 104.7 %collective-permute-start.1 = (bf16[768,512]{1,0:T(8,128)(2,1)S(1)}, bf16[768,512]{1,0:T(8,128)(2,1)}, u32[]{:S(2)}, u32[]{:S(2)}) collective-permute-start(bf16[768,512]{1,0:T(8,128)(2,1)S(1)} %bitcast_multiply_fusion.1), channel_id=1, source_target_pairs={{0,6},{2,8},{4,10},{6,12},{8,14},{10,16},{12,18},{14,20},{16,22},{... | collective-permute-start | bytes 2359304 | tf_op jit(solution)/shard_map/ppermute | solution.py:12
  18.0 103.6 %collective-permute-start.2 = (bf16[768,512]{1,0:T(8,128)(2,1)S(1)}, bf16[768,512]{1,0:T(8,128)(2,1)}, u32[]{:S(2)}, u32[]{:S(2)}) collective-permute-start(bf16[768,512]{1,0:T(8,128)(2,1)S(1)} %bitcast_multiply_fusion.1), channel_id=1, source_target_pairs={{0,4},{2,6},{4,8},{6,10},{8,12},{10,14},{12,16},{14,18},{16,20},{1... | collective-permute-start | bytes 2359304 | tf_op jit(solution)/shard_map/ppermute | solution.py:12
  21.4 102.9 %collective-permute-start.3 = (bf16[768,512]{1,0:T(8,128)(2,1)S(1)}, bf16[768,512]{1,0:T(8,128)(2,1)}, u32[]{:S(2)}, u32[]{:S(2)}) collective-permute-start(bf16[768,512]{1,0:T(8,128)(2,1)S(1)} %bitcast_multiply_fusion.1), channel_id=1, source_target_pairs={{0,2},{2,4},{4,6},{6,8},{8,10},{10,12},{12,14},{14,16},{16,18},{18... | collective-permute-start | bytes 2359304 | tf_op jit(solution)/shard_map/ppermute | solution.py:12
  24.0 101.8 %collective-permute-start.4 = (bf16[768,512]{1,0:T(8,128)(2,1)S(1)}, bf16[768,512]{1,0:T(8,128)(2,1)S(1)}, u32[]{:S(2)}, u32[]{:S(2)}) collective-permute-start(bf16[768,512]{1,0:T(8,128)(2,1)S(1)} %bitcast_multiply_fusion.1), channel_id=1, source_target_pairs={{2,0},{4,2},{6,4},{8,6},{10,8},{12,10},{14,12},{16,14},{18,16},{20... | collective-permute-start | bytes 2359304 | tf_op jit(solution)/shard_map/ppermute | solution.py:12
  116.6 54.1 %copy-start.4 = (s32[1,1,8]{2,1,0:T(1,128)S(1)}, s32[1,1,8]{2,1,0:T(1,128)}, u32[]{:S(2)}) copy-start(s32[1,1,8]{2,1,0:T(1,128)} %param.15) | copy-start | bytes 100
  116.6 22.3 %collective-permute-start.5 = (bf16[768,512]{1,0:T(8,128)(2,1)S(1)}, bf16[768,512]{1,0:T(8,128)(2,1)S(1)}, u32[]{:S(2)}, u32[]{:S(2)}) collective-permute-start(bf16[768,512]{1,0:T(8,128)(2,1)S(1)} %bitcast_multiply_fusion.1), channel_id=1, source_target_pairs={{4,0},{6,2},{8,4},{10,6},{12,8},{14,10},{16,12},{18,14},{20,16},{2... | collective-permute-start | bytes 2359304 | tf_op jit(solution)/shard_map/ppermute | solution.py:12
  119.1 25.3 %collective-permute-start.6 = (bf16[768,512]{1,0:T(8,128)(2,1)S(1)}, bf16[768,512]{1,0:T(8,128)(2,1)S(1)}, u32[]{:S(2)}, u32[]{:S(2)}) collective-permute-start(bf16[768,512]{1,0:T(8,128)(2,1)S(1)} %bitcast_multiply_fusion.1), channel_id=1, source_target_pairs={{6,0},{8,2},{10,4},{12,6},{14,8},{16,10},{18,12},{20,14},{22,16},{... | collective-permute-start | bytes 2359304 | tf_op jit(solution)/shard_map/ppermute | solution.py:12
  121.6 49.1 %collective-permute-start.7 = (bf16[768,512]{1,0:T(8,128)(2,1)S(1)}, bf16[768,512]{1,0:T(8,128)(2,1)S(1)}, u32[]{:S(2)}, u32[]{:S(2)}) collective-permute-start(bf16[768,512]{1,0:T(8,128)(2,1)S(1)} %bitcast_multiply_fusion.1), channel_id=1, source_target_pairs={{8,0},{10,2},{12,4},{14,6},{16,8},{18,10},{20,12},{22,14},{24,16},... | collective-permute-start | bytes 2359304 | tf_op jit(solution)/shard_map/ppermute | solution.py:12
  188.5 5.9 %copy-start.5 = (s32[1,1,7]{2,1,0:T(1,128)S(1)}, s32[1,1,7]{2,1,0:T(1,128)}, u32[]{:S(2)}) copy-start(s32[1,1,7]{2,1,0:T(1,128)} %param.16) | copy-start | bytes 88
  188.5 8.5 %copy-start.2 = (bf16[1,1,768,128]{3,2,1,0:T(8,128)(2,1)S(1)}, bf16[1,1,768,128]{3,2,1,0:T(8,128)(2,1)}, u32[]{:S(2)}) copy-start(bf16[1,1,768,128]{3,2,1,0:T(8,128)(2,1)} %param.11) | copy-start | bytes 589828
  188.5 8.5 %copy-start.3 = (bf16[1,1,128,128]{3,2,1,0:T(8,128)(2,1)S(1)}, bf16[1,1,128,128]{3,2,1,0:T(8,128)(2,1)}, u32[]{:S(2)}) copy-start(bf16[1,1,128,128]{3,2,1,0:T(8,128)(2,1)} %param.12) | copy-start | bytes 98308
Sparse Core Ops, SparseCore 0:
  27.8 49.3 all-gather.2
where the time goes:
time: 218 us; the launch traced here: 217 us
  blocking collectives  86 us (39%)
  waiting for transfers between devices  44.8 us (21%)
  matrix products  28.3 us (13%)
  local copies, waits for them, and re-layouts  21.5 us (10%)
  starting transfers between devices  20.7 us (9%)
  between operations  14.4 us (7%)
    psum x1, blocking collectives, body(): lax.psum(owner[:, None, None] * upward[None], ('leaf', 'top'))  86 us
    ppermute x8, waiting for transfers between devices, passed_along(): return lax.ppermute(block, axis, route)  44.8 us
    ppermute x8, starting transfers between devices, passed_along(): return lax.ppermute(block, axis, route)  20.7 us
    dot_general x1, matrix products, body(): jnp.einsum('kij,kjv->iv', tiles, sources.astype(jnp.bfloat16), preferred_...  10.2 us
    dot_general x1, local copies, waits for them, and re-layouts, body(): jnp.einsum('kw,wrv->krv', picker, stacked, preferred_element_type=jnp.flo...  9.06 us
    dot_general x1, matrix products, body(): jnp.einsum('kw,wrv->krv', picker, stacked, preferred_element_type=jnp.flo...  8.66 us
    unnamed x20, local copies, waits for them, and re-layouts  7.17 us
  transfers between devices with their start and end apart: 9, of which 3 were waited for; matrix products, arithmetic and copies ran while one was open for 13% of the time, Pallas kernels for 0%

commit v1 on v0

--- a/solution.py
+++ b/solution.py
@@ -50,7 +50,9 @@
     upward = jnp.einsum("ab,av->bv", nested, coeff, preferred_element_type=jnp.float32)
     clusters = lax.axis_size("top")
     owner = (jnp.arange(clusters, dtype=jnp.int32) == lax.axis_index("top")).astype(jnp.float32)
-    parents = lax.psum(owner[:, None, None] * upward[None], ("leaf", "top")).astype(jnp.bfloat16)
+    parents = lax.psum(lax.psum(owner[:, None, None] * upward[None], "top"), "leaf").astype(
+        jnp.bfloat16
+    )
     sibling_ids = (lax.axis_index("top") + 1 + jnp.arange(clusters, dtype=jnp.int32)) % clusters
     top_pick = (sibling_ids[:, None] == jnp.arange(clusters, dtype=jnp.int32)[None, :]).astype(
         jnp.bfloat16

time: 218 us -> 241 us (1.11)
  blocking collectives: 86 us -> 99 us
  waiting for transfers between devices: 44.8 us -> 54.4 us
    psum x0 -> x1, waiting for transfers between devices: none -> 14.2 us  [body(): lax.psum(owner[:, None, None] * upward[None], 'top')]
    psum x1, blocking collectives: 86 us -> 99 us  [body(): lax.psum(lax.psum(owner[:, None, None] * upward[None], 'top'), 'leaf')]
    ppermute x8, waiting for transfers between devices: 44.8 us -> 40.1 us  [passed_along(): return lax.ppermute(block, axis, route)]
    unnamed x20 -> x22, local copies, waits for them, and re-layouts: 7.17 us -> 6.05 us
  transfers between devices with their start and end apart: 9 -> 10, of which waited for: 3 -> 4; matrix products, arithmetic and copies ran while one was open for 13% -> 11% of each run, Pallas kernels for 0% -> 0%
where the time goes in v1:
time: 241 us; the launch traced here: 240 us
  blocking collectives  99 us (41%)
  waiting for transfers between devices  54.4 us (23%)
  matrix products  28.5 us (12%)
  local copies, waits for them, and re-layouts  20.3 us (8%)
  starting transfers between devices  19.9 us (8%)
  between operations  15.9 us (7%)
  other arithmetic  2.48 us (1%)
    psum x1, blocking collectives, body(): lax.psum(lax.psum(owner[:, None, None] * upward[None], 'top'), 'leaf')  99 us
    ppermute x8, waiting for transfers between devices, passed_along(): return lax.ppermute(block, axis, route)  40.1 us
    ppermute x8, starting transfers between devices, passed_along(): return lax.ppermute(block, axis, route)  19.9 us
    psum x1, waiting for transfers between devices, body(): lax.psum(owner[:, None, None] * upward[None], 'top')  14.2 us
    dot_general x1, matrix products, body(): jnp.einsum('kij,kjv->iv', tiles, sources.astype(jnp.bfloat16), preferred_...  10.2 us
    dot_general x1, local copies, waits for them, and re-layouts, body(): jnp.einsum('kw,wrv->krv', picker, stacked, preferred_element_type=jnp.flo...  9.05 us
    dot_general x1, matrix products, body(): jnp.einsum('kw,wrv->krv', picker, stacked, preferred_element_type=jnp.flo...  8.67 us
    unnamed x22, local copies, waits for them, and re-layouts  6.05 us
  transfers between devices with their start and end apart: 10, of which 4 were waited for; matrix products, arithmetic and copies ran while one was open for 11% of the time, Pallas kernels for 0%

profile of v1, /device:TPU:0, one launch (start us, length us, event | category | flops | bytes accessed | tf_op | source)
XLA Modules:
  0.0 240.5 jit_solution(8750324200065911623)
XLA Ops:
  8.1 1.7 convolution_convert_fusion
  9.9 1.0 convolution_bitcast_fusion.1
  10.9 0.9 broadcast_multiply_fusion
  11.9 1.3 bitcast_multiply_fusion.1
  13.2 5.9 %collective-permute-start = (bf16[768,512]{1,0:T(8,128)(2,1)S(1)}, bf16[768,512]{1,0:T(8,128)(2,1)}, u32[]{:S(2)}, u32[]{:S(2)}) collective-permute-start(bf16[768,512]{1,0:T(8,128)(2,1)S(1)} %bitcast_multiply_fusion.1), channel_id=1, source_target_pairs={{0,8},{2,10},{4,12},{6,14},{8,16},{10,18},{12,20},{14,22},{16,24},... | collective-permute-start | bytes 2359304 | tf_op jit(solution)/shard_map/ppermute | solution.py:12
  19.1 3.5 %collective-permute-start.1 = (bf16[768,512]{1,0:T(8,128)(2,1)S(1)}, bf16[768,512]{1,0:T(8,128)(2,1)}, u32[]{:S(2)}, u32[]{:S(2)}) collective-permute-start(bf16[768,512]{1,0:T(8,128)(2,1)S(1)} %bitcast_multiply_fusion.1), channel_id=1, source_target_pairs={{0,6},{2,8},{4,10},{6,12},{8,14},{10,16},{12,18},{14,20},{16,22},{... | collective-permute-start | bytes 2359304 | tf_op jit(solution)/shard_map/ppermute | solution.py:12
  22.6 3.4 %collective-permute-start.2 = (bf16[768,512]{1,0:T(8,128)(2,1)S(1)}, bf16[768,512]{1,0:T(8,128)(2,1)}, u32[]{:S(2)}, u32[]{:S(2)}) collective-permute-start(bf16[768,512]{1,0:T(8,128)(2,1)S(1)} %bitcast_multiply_fusion.1), channel_id=1, source_target_pairs={{0,4},{2,6},{4,8},{6,10},{8,12},{10,14},{12,16},{14,18},{16,20},{1... | collective-permute-start | bytes 2359304 | tf_op jit(solution)/shard_map/ppermute | solution.py:12
  26.0 1.8 collective-permute-start.3
  27.8 1.3 collective-permute-start.4
  29.2 14.2 %all-reduce.3.cloned.1.call-done = f32[2,128,512]{2,1,0:T(8,128)} async-done(((f32[2,128,512]{2,1,0:T(8,128)}), f32[2,128,512]{2,1,0:T(8,128)}) %all-reduce.3.cloned.1.call-update) | async-done | bytes 524304 | tf_op jit(solution)/shard_map/psum | solution.py:53
  43.4 99.0 %all-reduce.4 = bf16[2,128,512]{2,1,0:T(8,128)(2,1)} all-reduce(f32[2,128,512]{2,1,0:T(8,128)} %all-reduce.3.cloned.1.call-done), channel_id=1, replica_groups=mesh['leaf'=16,'top'=2] {'leaf'}, use_global_device_ids=true, to_apply=%region_1.0 | all-reduce | flops 131072 | bytes 786432 | tf_op jit(solution)/shard_map/psum | solution.py:53
  142.4 1.4 fusion.18
  143.8 1.1 fusion.11
  144.9 1.3 collective-permute-start.5
  146.2 1.2 bitcast_dynamic-update-slice_fusion.7
  147.4 1.3 collective-permute-start.6
  148.7 1.2 bitcast_dynamic-update-slice_fusion.6
  149.9 1.5 collective-permute-start.7
  151.4 1.2 bitcast_dynamic-update-slice_fusion.5
  152.7 0.2 fusion.15
  153.0 14.3 %collective-permute-done.5 = bf16[768,512]{1,0:T(8,128)(2,1)S(1)} collective-permute-done((bf16[768,512]{1,0:T(8,128)(2,1)S(1)}, bf16[768,512]{1,0:T(8,128)(2,1)S(1)}, u32[]{:S(2)}, u32[]{:S(2)}) %collective-permute-start.5) | collective-permute-done | bytes 786464 | tf_op jit(solution)/shard_map/ppermute | solution.py:12
  167.3 3.5 %collective-permute-done.6 = bf16[768,512]{1,0:T(8,128)(2,1)S(1)} collective-permute-done((bf16[768,512]{1,0:T(8,128)(2,1)S(1)}, bf16[768,512]{1,0:T(8,128)(2,1)S(1)}, u32[]{:S(2)}, u32[]{:S(2)}) %collective-permute-start.6) | collective-permute-done | bytes 786464 | tf_op jit(solution)/shard_map/ppermute | solution.py:12
  170.8 22.4 %collective-permute-done.7 = bf16[768,512]{1,0:T(8,128)(2,1)S(1)} collective-permute-done((bf16[768,512]{1,0:T(8,128)(2,1)S(1)}, bf16[768,512]{1,0:T(8,128)(2,1)S(1)}, u32[]{:S(2)}, u32[]{:S(2)}) %collective-permute-start.7) | collective-permute-done | bytes 786464 | tf_op jit(solution)/shard_map/ppermute | solution.py:12
  193.3 8.7 %fusion = bf16[8,768,512]{2,0,1:T(8,128)(2,1)} fusion(bf16[9,768,512]{2,1,0:T(8,128)(2,1)S(1)} %bitcast_dynamic-update-slice_fusion, s32[9]{0:T(128)S(1)} %iota_add_fusion, s32[8]{0:T(128)S(1)} %bitcast.91), kind=kOutput, calls=%fused_computation | convolution fusion | flops 56623176 | bytes 13369412 | tf_op jit(solution)/shard_map/kw,wrv->krv/dot_general | solution.py:41
  201.9 9.1 %copy.12 = bf16[8,768,512]{1,2,0:T(8,128)(2,1)} copy(bf16[8,768,512]{2,0,1:T(8,128)(2,1)} %fusion) | data formatting | bytes 12582912 | tf_op jit(solution)/shard_map/kw,wrv->krv/dot_general | solution.py:41
  211.0 2.3 copy.17
  213.3 3.6 %copy.13 = bf16[16,128,512]{2,0,1:T(8,128)(2,1)} copy(bf16[16,128,512]{1,0,2:T(8,128)(2,1)S(1)} %bitcast.88) | data formatting | bytes 4194304 | tf_op jit(solution)/shard_map/all_gather | solution.py:68
  216.8 2.1 fusion.29
  218.9 0.6 convolution_bitcast_fusion.2
  219.5 1.7 fusion.13
  221.2 10.2 %fusion.6 = f32[1,1,768,512]{2,3,1,0:T(8,128)S(1)} fusion(f32[512,768]{1,0:T(8,128)} %fusion.13, bf16[1,1,8,768,768]{4,3,2,1,0:T(8,128)(2,1)} %param.10, bf16[8,768,512]{1,2,0:T(8,128)(2,1)} %copy.12, f32[768]{0:T(1024)S(1)} %fusion.37), kind=kOutput, calls=%fused_computation.8 | convolution fusion | flops 4832624640 | bytes 18877440 | tf_op jit(solution)/shard_map/kij,kjv->iv/dot_general | solution.py:42
  231.4 1.6 copy.10
  (34 shorter events, 0.4 us)
Async XLA Ops:
  7.4 211.6 %copy-start = (bf16[1,1,7,128,128]{4,3,2,1,0:T(8,128)(2,1)S(1)}, bf16[1,1,7,128,128]{4,3,2,1,0:T(8,128)(2,1)}, u32[]{:S(2)}) copy-start(bf16[1,1,7,128,128]{4,3,2,1,0:T(8,128)(2,1)} %param.13) | copy-start | bytes 688132
  7.4 145.3 %copy-start.1 = (bf16[1,1,768,512]{3,2,1,0:T(8,128)(2,1)S(1)}, bf16[1,1,768,512]{3,2,1,0:T(8,128)(2,1)}, u32[]{:S(2)}) copy-start(bf16[1,1,768,512]{3,2,1,0:T(8,128)(2,1)} %param.9) | copy-start | bytes 2359300
  7.4 36.0 %all-reduce.3.cloned.1.call-start = ((), (), s32[]{:S(2)}) async-start(), calls=%async_computation | async-start | bytes 1048576 | tf_op jit(solution)/shard_map/psum | solution.py:53
  9.9 19.2 %copy-start.2 = (bf16[512,128]{1,0:T(8,128)(2,1)}, bf16[512,128]{1,0:T(8,128)(2,1)S(1)}, u32[]{:S(2)}) copy-start(bf16[512,128]{1,0:T(8,128)(2,1)S(1)} %convolution_convert_fusion) | copy-start | bytes 393220
  11.9 199.2 %all-gather.3.cloned.1.call-start = ((), (), s32[]{:S(2)}) async-start(), calls=%async_computation.1 | async-start | bytes 2228224 | tf_op jit(solution)/shard_map/all_gather | solution.py:68
  13.2 131.7 %collective-permute-start = (bf16[768,512]{1,0:T(8,128)(2,1)S(1)}, bf16[768,512]{1,0:T(8,128)(2,1)}, u32[]{:S(2)}, u32[]{:S(2)}) collective-permute-start(bf16[768,512]{1,0:T(8,128)(2,1)S(1)} %bitcast_multiply_fusion.1), channel_id=1, source_target_pairs={{0,8},{2,10},{4,12},{6,14},{8,16},{10,18},{12,20},{14,22},{16,24},... | collective-permute-start | bytes 2359304 | tf_op jit(solution)/shard_map/ppermute | solution.py:12
  19.1 128.3 %collective-permute-start.1 = (bf16[768,512]{1,0:T(8,128)(2,1)S(1)}, bf16[768,512]{1,0:T(8,128)(2,1)}, u32[]{:S(2)}, u32[]{:S(2)}) collective-permute-start(bf16[768,512]{1,0:T(8,128)(2,1)S(1)} %bitcast_multiply_fusion.1), channel_id=1, source_target_pairs={{0,6},{2,8},{4,10},{6,12},{8,14},{10,16},{12,18},{14,20},{16,22},{... | collective-permute-start | bytes 2359304 | tf_op jit(solution)/shard_map/ppermute | solution.py:12
  22.6 127.3 %collective-permute-start.2 = (bf16[768,512]{1,0:T(8,128)(2,1)S(1)}, bf16[768,512]{1,0:T(8,128)(2,1)}, u32[]{:S(2)}, u32[]{:S(2)}) collective-permute-start(bf16[768,512]{1,0:T(8,128)(2,1)S(1)} %bitcast_multiply_fusion.1), channel_id=1, source_target_pairs={{0,4},{2,6},{4,8},{6,10},{8,12},{10,14},{12,16},{14,18},{16,20},{1... | collective-permute-start | bytes 2359304 | tf_op jit(solution)/shard_map/ppermute | solution.py:12
  26.0 126.6 %collective-permute-start.3 = (bf16[768,512]{1,0:T(8,128)(2,1)S(1)}, bf16[768,512]{1,0:T(8,128)(2,1)S(1)}, u32[]{:S(2)}, u32[]{:S(2)}) collective-permute-start(bf16[768,512]{1,0:T(8,128)(2,1)S(1)} %bitcast_multiply_fusion.1), channel_id=1, source_target_pairs={{0,2},{2,4},{4,6},{6,8},{8,10},{10,12},{12,14},{14,16},{16,18},{18... | collective-permute-start | bytes 2359304 | tf_op jit(solution)/shard_map/ppermute | solution.py:12
  27.8 125.1 %collective-permute-start.4 = (bf16[768,512]{1,0:T(8,128)(2,1)S(1)}, bf16[768,512]{1,0:T(8,128)(2,1)S(1)}, u32[]{:S(2)}, u32[]{:S(2)}) collective-permute-start(bf16[768,512]{1,0:T(8,128)(2,1)S(1)} %bitcast_multiply_fusion.1), channel_id=1, source_target_pairs={{2,0},{4,2},{6,4},{8,6},{10,8},{12,10},{14,12},{16,14},{18,16},{20... | collective-permute-start | bytes 2359304 | tf_op jit(solution)/shard_map/ppermute | solution.py:12
  144.9 48.3 %copy-start.5 = (s32[1,1,8]{2,1,0:T(1,128)S(1)}, s32[1,1,8]{2,1,0:T(1,128)}, u32[]{:S(2)}) copy-start(s32[1,1,8]{2,1,0:T(1,128)} %param.15) | copy-start | bytes 100
  144.9 22.3 %collective-permute-start.5 = (bf16[768,512]{1,0:T(8,128)(2,1)S(1)}, bf16[768,512]{1,0:T(8,128)(2,1)S(1)}, u32[]{:S(2)}, u32[]{:S(2)}) collective-permute-start(bf16[768,512]{1,0:T(8,128)(2,1)S(1)} %bitcast_multiply_fusion.1), channel_id=1, source_target_pairs={{4,0},{6,2},{8,4},{10,6},{12,8},{14,10},{16,12},{18,14},{20,16},{2... | collective-permute-start | bytes 2359304 | tf_op jit(solution)/shard_map/ppermute | solution.py:12
  147.4 23.3 %collective-permute-start.6 = (bf16[768,512]{1,0:T(8,128)(2,1)S(1)}, bf16[768,512]{1,0:T(8,128)(2,1)S(1)}, u32[]{:S(2)}, u32[]{:S(2)}) collective-permute-start(bf16[768,512]{1,0:T(8,128)(2,1)S(1)} %bitcast_multiply_fusion.1), channel_id=1, source_target_pairs={{6,0},{8,2},{10,4},{12,6},{14,8},{16,10},{18,12},{20,14},{22,16},{... | collective-permute-start | bytes 2359304 | tf_op jit(solution)/shard_map/ppermute | solution.py:12
  149.9 43.3 %collective-permute-start.7 = (bf16[768,512]{1,0:T(8,128)(2,1)S(1)}, bf16[768,512]{1,0:T(8,128)(2,1)S(1)}, u32[]{:S(2)}, u32[]{:S(2)}) collective-permute-start(bf16[768,512]{1,0:T(8,128)(2,1)S(1)} %bitcast_multiply_fusion.1), channel_id=1, source_target_pairs={{8,0},{10,2},{12,4},{14,6},{16,8},{18,10},{20,12},{22,14},{24,16},... | collective-permute-start | bytes 2359304 | tf_op jit(solution)/shard_map/ppermute | solution.py:12
  211.0 5.9 %copy-start.6 = (s32[1,1,7]{2,1,0:T(1,128)S(1)}, s32[1,1,7]{2,1,0:T(1,128)}, u32[]{:S(2)}) copy-start(s32[1,1,7]{2,1,0:T(1,128)} %param.16) | copy-start | bytes 88
  211.0 8.5 %copy-start.3 = (bf16[1,1,768,128]{3,2,1,0:T(8,128)(2,1)S(1)}, bf16[1,1,768,128]{3,2,1,0:T(8,128)(2,1)}, u32[]{:S(2)}) copy-start(bf16[1,1,768,128]{3,2,1,0:T(8,128)(2,1)} %param.11) | copy-start | bytes 589828
  211.0 8.5 %copy-start.4 = (bf16[1,1,128,128]{3,2,1,0:T(8,128)(2,1)S(1)}, bf16[1,1,128,128]{3,2,1,0:T(8,128)(2,1)}, u32[]{:S(2)}) copy-start(bf16[1,1,128,128]{3,2,1,0:T(8,128)(2,1)} %param.12) | copy-start | bytes 98308
Sparse Core Ops, SparseCore 0:
  12.0 31.3 all-reduce.2
Sparse Core Ops, SparseCore 1:
  29.2 51.8 all-gather.2
